TPU v7x, 256 devices: a 2x2x32 block of a 4x8x32 slice. The times are simulated.
256 devices in a mesh: grp: 4 (over x, y), tp: 32 (over z), tower: 2 (over core).
Axes of the slice: x: 2, y: 2, z: 32, core: 2. Of those that a mesh axis runs over, the one named last changes fastest.
The devices are a block of a 4x8x32 slice.
Arguments:
- hidden: bfloat16 [2, 4096, 3072], P('tower', ('grp', 'tp')), parts along dimension 1, may hold values from -6 to 6
- modulation: float32 [2, 3, 3072], P('tower'), may hold values from -3 to 7, as said below
- qk_gains: float32 [2, 3, 4096], P('tower', None, 'tp'), may hold values from 0.75 to 13
- counts: int32 [2, 4], P(None, 'grp'), parts along dimension 1, may hold values from 256 to 1024
- offsets: int32 [2, 4], P(None, 'grp'), parts along dimension 1, may hold values from 0 to 8191
- in_weights: bfloat16 [2, 3072, 4, 4096], P('tower', None, None, 'tp'), may hold values from -0.109375 to 0.109375
- out_weights: bfloat16 [2, 2, 4096, 3072], P('tower', None, 'tp'), may hold values from -0.5 to 0.5
Outputs:
- updated: bfloat16 [2, 4096, 3072], P('tower', ('grp', 'tp')), parts along dimension 1
There are 4 independent parts, one for each index of `grp`. A program takes and returns all parts, laid end to end along the dimension named above; an argument that names none is the same for every part. Nothing has to cross between parts.
Inputs may be any that keep to these rules, and one draw needn't show every extreme that they name: `modulation`: rows are shift, scale and gate.
All inputs are finite; a program needn't handle non-finite values.
Results may differ from a plain program's by a relative error of at most 0.025.
The roundings to bfloat16 on the way count: a program that leaves them out, or rounds other values in their place, can miss the bound.
Values may be sent and summed in bfloat16 or wider, within the bound.
No kernel may reach another device: no remote copies, remote signals or barrier semaphores. Data moves between devices by JAX's collectives and lax.ppermute only.
A program may use at most 64 MiB of HBM per device.

v0:
```python
import math
import jax
import jax.numpy as jnp
from jax import lax
from jax.sharding import PartitionSpec as P

epsilon = 1e-06
rope_base = 10000.0
masked_score = -1e30


def partner(value, axis, distance):
    mask = 2**distance
    pairs = [(source, source ^ mask) for source in range(lax.axis_size(axis))]
    return lax.ppermute(value, axis, pairs)


def layer_norm(states):
    centre = states - jnp.mean(states, -1, keepdims=True)
    spread = jnp.mean(centre * centre, -1, keepdims=True)
    return centre * lax.rsqrt(spread + epsilon)


def rotate(columns, positions):
    head_width = columns.shape[-1]
    pair_index = jnp.arange(head_width // 2, dtype=jnp.int32)
    frequency = jnp.exp(pair_index.astype(jnp.float32) * (-2.0 * math.log(rope_base) / head_width))
    angles = positions.reshape((positions.shape[0],) + (1,) * (columns.ndim - 1)) * frequency
    cosine = jnp.cos(angles)
    sine_table = jnp.sin(angles)
    even_part = columns[..., 0::2]
    odd_part = columns[..., 1::2]
    turned = jnp.stack(
        [even_part * cosine - odd_part * sine_table, even_part * sine_table + odd_part * cosine], -1
    )
    return turned.reshape(columns.shape)


def finish(projected, head_gains, positions):
    query_like = jnp.stack([projected[:, 0], projected[:, 1], projected[:, 3]], 1)
    squares = jnp.mean(query_like * query_like, -1, keepdims=True)
    query_like = query_like * lax.rsqrt(squares + epsilon) * head_gains[None]
    turned = rotate(query_like, positions)
    return jnp.stack([turned[:, 0], turned[:, 1], projected[:, 2], turned[:, 2]], 1)


def attend(queries, key_rows, value_rows, key_count):
    scores = jnp.einsum("qd,kd->qk", queries, key_rows, preferred_element_type=jnp.float32) * (
        1.0 / math.sqrt(queries.shape[-1])
    )
    usable = jnp.arange(key_rows.shape[0], dtype=jnp.int32) < key_count
    scores = jnp.where(usable[None, :], scores, masked_score)
    row_max = jnp.max(scores, -1, keepdims=True)
    raised = jnp.exp(scores - row_max)
    attention = (raised / jnp.sum(raised, -1, keepdims=True)).astype(jnp.bfloat16)
    return jnp.dot(attention, value_rows, preferred_element_type=jnp.float32).astype(jnp.bfloat16)


def attend_blocks(queries, key_rows, value_rows, key_count):
    row_count = queries.shape[0]
    block_rows = min(512, row_count)
    grouped = queries.reshape(row_count // block_rows, block_rows, queries.shape[-1])
    result = lax.map(
        lambda query_block: attend(query_block, key_rows, value_rows, key_count), grouped
    )
    return result.reshape(row_count, queries.shape[-1])


def local(hidden, modulation, qk_gains, counts, offsets, in_weights, out_weights):
    states = hidden[0].astype(jnp.float32)
    modulate = modulation[0]
    normed = (layer_norm(states) * (1.0 + modulate[1]) + modulate[0]).astype(jnp.bfloat16)
    local_rows = states.shape[0]
    model_width = normed.shape[1]
    all_rows = local_rows * lax.axis_size("tp")
    tower_index = lax.axis_index("tower")
    own_count = lax.dynamic_index_in_dim(counts[:, 0], tower_index, 0, False)
    own_offset = lax.dynamic_index_in_dim(offsets[:, 0], tower_index, 0, False)
    head_width = in_weights.shape[-1]
    flat_weights = in_weights[0].reshape(model_width, 4 * head_width)
    head_gains = qk_gains[0].reshape(3, 1, head_width)
    row_piece = lax.all_gather(normed, "tp", axis=0, tiled=True)
    row_count = row_piece.shape[0]
    projected = jnp.dot(row_piece, flat_weights, preferred_element_type=jnp.float32).reshape(
        row_count, 4, 1, head_width
    )
    positions = (own_offset + jnp.arange(row_count, dtype=jnp.int32)).astype(jnp.float32)
    finished = finish(projected, head_gains, positions)
    projected = (
        finished.astype(jnp.bfloat16)
        .reshape(row_count, 4 * head_width)
        .reshape(all_rows, 4, head_width)
    )
    queries = projected[:, 0]
    key_rows = projected[:, 1]
    value_rows = projected[:, 2]
    cross_queries = projected[:, 3]
    self_out = attend_blocks(queries, key_rows, value_rows, own_count)
    foreign = partner(cross_queries, "tower", 0)
    answered = attend_blocks(foreign, key_rows, value_rows, own_count)
    cross_out = partner(answered, "tower", 0)
    both_out = jnp.concatenate([self_out, cross_out], 1)
    flat_out = out_weights[0].reshape(2 * head_width, model_width)
    branch = lax.psum_scatter(
        jnp.dot(both_out, flat_out, preferred_element_type=jnp.float32).astype(jnp.bfloat16),
        "tp",
        scatter_dimension=0,
        tiled=True,
    ).astype(jnp.float32)
    return (states + modulate[2] * branch).astype(jnp.bfloat16)[None]


def solution(mesh):
    return jax.shard_map(
        local,
        mesh=mesh,
        in_specs=(
            P("tower", ("grp", "tp"), None),
            P("tower", None, None),
            P("tower", None, "tp"),
            P(None, "grp"),
            P(None, "grp"),
            P("tower", None, None, "tp"),
            P("tower", None, "tp", None),
        ),
        out_specs=P("tower", ("grp", "tp"), None),
        check_vma=False,
    )
```

profile of v0, /device:TPU:38, one launch (start us, length us, event | category | flops | bytes accessed | tf_op | source)
XLA Modules:
  0.0 345.4 jit_solution(10798262315295197064)
XLA Ops:
  6.6 0.9 fusion.41
  7.4 1.1 convert_reduce_fusion
  8.5 1.2 fusion.32
  9.7 1.8 fusion.35
  11.6 4.1 %copy.25 = bf16[384,8,4,128]{3,1,2,0:T(8,128)(2,1)} copy(bf16[384,8,4,128]{3,2,1,0:T(4,128)(2,1)} %bitcast.111) | data formatting | bytes 6291456
  15.6 4.8 %copy.11 = bf16[512,3072]{1,0:T(8,128)(2,1)} copy(bf16[512,3072]{0,1:T(8,128)(2,1)} %bitcast.108) | data formatting | bytes 6291456 | tf_op jit(solution)/shard_map/dot_general | solution.py:84
  20.4 0.7 constant_dynamic-slice_fusion.1
  21.1 0.6 constant_dynamic-slice_fusion
  21.7 0.6 add_convert_fusion
  22.3 1.8 multiply_cosine_fusion
  24.1 142.7 %all-gather.2.cloned.1.call-done = bf16[1024,3072]{1,0:T(8,128)(2,1)} async-done(((bf16[32,3072]{1,0:T(8,128)(2,1)}), bf16[1024,3072]{1,0:T(8,128)(2,1)}) %all-gather.2.cloned.1.call-update) | async-done | bytes 6291472 | tf_op jit(solution)/shard_map/all_gather | solution.py:82
  166.8 6.5 %fusion.22 = f32[1024,4,1,128]{0,3,1,2:T(8,128)S(1)} fusion(bf16[4,128,3072]{2,1,0:T(8,128)(2,1)} %bitcast.112, bf16[1024,3072]{1,0:T(8,128)(2,1)} %all-gather.2.cloned.1.call-done), kind=kOutput, calls=%fused_computation.34 | convolution fusion | flops 3221225472 | bytes 11534336 | tf_op jit(solution)/shard_map/dot_general | solution.py:84
  173.5 0.2 multiply_reduce_fusion
  173.6 1.1 copy-done.2
  174.7 0.2 multiply_multiply_fusion
  174.9 2.2 slice.56
  177.1 2.1 slice.55
  179.2 1.7 subtract_bitcast_fusion
  181.0 0.8 copy.12
  181.8 0.3 reshape.237
  182.2 0.1 collective-permute-start
  182.4 0.2 copy.14
  182.6 1.1 fusion.37
  183.6 0.2 copy.15
  183.8 0.2 copy.19
  184.0 0.2 copy.20
  184.2 5.1 %while.21 = (s32[]{:T(128)}, bf16[2,512,128]{2,1,0:T(8,128)(2,1)S(1)}, s32[]{:T(128)}, bf16[2,512,128]{2,1,0:T(8,128)(2,1)S(1)}, bf16[1024,128]{1,0:T(8,128)(2,1)S(1)}, /*index=5*/bf16[1024,128]{1,0:T(8,128)(2,1)S(1)}, s32[]{:T(128)}) while((s32[]{:T(128)}, bf16[2,512,128]{2,1,0:T(8,128)(2,1)S(1)}, s32[]{:T(128)}, ...), condition=%wide.region_10.11_spmd, body=%wide.region_7.10_spmd.sunk | while | flops 274792448 | bytes 7092321 | solution.py:63
  184.2 0.7 iota_compare_fusion.5
  184.9 0.5 fusion.65
  185.5 0.6 fusion.66
  186.1 0.7 fusion.67
  186.8 0.7 iota_compare_fusion.5
  187.5 0.5 fusion.65
  188.0 0.6 fusion.66
  188.6 0.7 fusion.67
  189.3 0.8 collective-permute-start.1
  190.2 5.1 %while.20 = (s32[]{:T(128)}, bf16[2,512,128]{2,1,0:T(8,128)(2,1)S(1)}, s32[]{:T(128)}, bf16[2,512,128]{2,1,0:T(8,128)(2,1)S(1)}, bf16[1024,128]{1,0:T(8,128)(2,1)S(1)}, /*index=5*/bf16[1024,128]{1,0:T(8,128)(2,1)S(1)}, s32[]{:T(128)}) while((s32[]{:T(128)}, bf16[2,512,128]{2,1,0:T(8,128)(2,1)S(1)}, s32[]{:T(128)}, ...), condition=%wide.region_6.7_spmd, body=%wide.region_3.6_spmd.sunk | while | flops 274792448 | bytes 7092321 | solution.py:63
  190.2 0.7 iota_compare_fusion.4
  190.9 0.5 fusion.60
  191.4 0.6 fusion.61
  192.0 0.7 fusion.62
  192.7 0.7 iota_compare_fusion.4
  193.4 0.5 fusion.60
  193.9 0.6 fusion.61
  194.5 0.7 fusion.62
  195.3 4.5 %convolution_convert_fusion.2 = bf16[1024,3072]{1,0:T(8,128)(2,1)} fusion(bf16[256,3072]{1,0:T(8,128)(2,1)S(1)} %bitcast.107, bf16[1024,128]{1,0:T(8,128)(2,1)S(1)} %collective-permute-done.1, bf16[1024,128]{1,0:T(8,128)(2,1)S(1)} %bitcast.113), kind=kOutput, calls=%fused_computation.32 | convolution fusion | flops 1614807040 | bytes 8388608 | tf_op jit(solution)/shard_map/dot_general | solution.py:105
  199.8 137.0 %reduce-scatter.2.cloned.1.call-done = bf16[32,3072]{1,0:T(8,128)(2,1)} async-done(((bf16[1024,3072]{1,0:T(8,128)(2,1)}), bf16[32,3072]{1,0:T(8,128)(2,1)}) %reduce-scatter.2.cloned.1.call-update) | async-done | bytes 196624 | tf_op jit(solution)/shard_map/reduce_scatter | solution.py:104
  336.9 1.7 fusion.38
  (30 shorter events, 0.6 us)
Async XLA Ops:
  6.5 188.7 %copy-start = (bf16[1,2,128,3072]{3,2,1,0:T(8,128)(2,1)S(1)}, bf16[1,2,128,3072]{3,2,1,0:T(8,128)(2,1)}, u32[]{:S(2)}) copy-start(bf16[1,2,128,3072]{3,2,1,0:T(8,128)(2,1)} %param.17) | copy-start | bytes 4718596
  6.6 160.3 %all-gather.2.cloned.1.call-start = ((), (), s32[]{:S(2)}) async-start(), calls=%async_computation.1 | async-start | bytes 6488064 | tf_op jit(solution)/shard_map/all_gather | solution.py:82
  11.5 325.4 %reduce-scatter.2.cloned.1.call-start = ((), (), s32[]{:S(2)}) async-start(), calls=%async_computation.2 | async-start | bytes 6488064 | tf_op jit(solution)/shard_map/reduce_scatter | solution.py:104
  15.6 4.8 %copy-start.3 = (f32[1,3,128]{2,0,1:T(1,128)S(1)}, f32[1,3,128]{2,0,1:T(1,128)}, u32[]{:S(2)}) copy-start(f32[1,3,128]{2,0,1:T(1,128)} %param.13) | copy-start | bytes 4612
  15.6 4.8 %copy-start.4 = (s32[2,1]{0,1:T(1,128)S(1)}, s32[2,1]{0,1:T(1,128)}, u32[]{:S(2)}) copy-start(s32[2,1]{0,1:T(1,128)} %param.14) | copy-start | bytes 28
  15.6 5.5 %copy-start.5 = (s32[2,1]{0,1:T(1,128)S(1)}, s32[2,1]{0,1:T(1,128)}, u32[]{:S(2)}) copy-start(s32[2,1]{0,1:T(1,128)} %param.15) | copy-start | bytes 28
  173.4 1.4 copy-start.2
  182.2 1.8 collective-permute-start
  189.3 5.9 %collective-permute-start.1 = (bf16[1024,128]{1,0:T(8,128)(2,1)S(1)}, bf16[1024,128]{1,0:T(8,128)(2,1)S(1)}, u32[]{:S(2)}, u32[]{:S(2)}) collective-permute-start(bf16[1024,128]{1,0:T(8,128)(2,1)S(1)} %bitcast.114), channel_id=1, source_target_pairs={{0,1},{1,0},{2,3},{3,2},{4,5},{5,4},{6,7},{7,6},{8,9},{9,8},{10,11... | collective-permute-start | bytes 786440 | tf_op jit(solution)/shard_map/ppermute | solution.py:15
  199.7 137.1 %copy-start.1 = (bf16[1,32,3072]{2,1,0:T(8,128)(2,1)S(1)}, bf16[1,32,3072]{2,1,0:T(8,128)(2,1)}, u32[]{:S(2)}) copy-start(bf16[1,32,3072]{2,1,0:T(8,128)(2,1)} %param.11) | copy-start | bytes 589828
Sparse Core Ops, SparseCore 0:
  11.6 155.1 all-gather.1
  199.9 136.8 reduce-scatter.1
where the time goes:
time: 346 us; the launch traced here: 345 us
  waiting for transfers between devices  280 us (81%)
  local copies, waits for them, and re-layouts  18.6 us (5%)
  other arithmetic  16.2 us (5%)
  matrix products  16 us (5%)
  between operations  13.6 us (4%)
    all_gather x1, waiting for transfers between devices, local(): row_piece = lax.all_gather(normed, 'tp', axis=0, tiled=True)  143 us
    reduce_scatter x1, waiting for transfers between devices, local(): lax.psum_scatter(jnp.dot(both_out, flat_out, preferred_element_type=jnp.f...  137 us
  transfers between devices with their start and end apart: 4, of which 2 were waited for; matrix products, arithmetic and copies ran while one was open for 6% of the time, Pallas kernels for 0%

commit v1 on v0

--- a/solution.py
+++ b/solution.py
@@ -79,7 +79,12 @@
     head_width = in_weights.shape[-1]
     flat_weights = in_weights[0].reshape(model_width, 4 * head_width)
     head_gains = qk_gains[0].reshape(3, 1, head_width)
-    row_piece = lax.all_gather(normed, "tp", axis=0, tiled=True)
+    axis_total = lax.axis_size("tp")
+    pool = []
+    for tick in tuple(range(normed.ndim)):
+        pool.append(axis_total if tick == 0 else 1)
+    built = jnp.tile(normed, pool)
+    row_piece = lax.all_to_all(built, "tp", split_axis=0, concat_axis=0, tiled=True)
     row_count = row_piece.shape[0]
     projected = jnp.dot(row_piece, flat_weights, preferred_element_type=jnp.float32).reshape(
         row_count, 4, 1, head_width

time: 346 us -> 776 us (2.24)
  waiting for transfers between devices: 280 us -> 674 us
  starting transfers between devices: 0.99 us -> 33.7 us
    all_to_all x0 -> x1, waiting for transfers between devices: none -> 532 us  [local(): lax.all_to_all(built, 'tp', split_axis=0, concat_axis=0, tiled=True)]
    all_gather x1 -> x0, waiting for transfers between devices: 143 us -> none  [local(): row_piece = lax.all_gather(normed, 'tp', axis=0, tiled=True)]
    all_to_all x0 -> x1, starting transfers between devices: none -> 32.7 us  [local(): lax.all_to_all(built, 'tp', split_axis=0, concat_axis=0, tiled=True)]
  transfers between devices with their start and end apart: 4 -> 4, of which waited for: 2 -> 2; matrix products, arithmetic and copies ran while one was open for 6% -> 2% of each run, Pallas kernels for 0% -> 0%
where the time goes in v1:
time: 776 us; the launch traced here: 775 us
  waiting for transfers between devices  674 us (87%)
  starting transfers between devices  33.7 us (4%)
  local copies, waits for them, and re-layouts  22 us (3%)
  matrix products  16 us (2%)
  other arithmetic  15.2 us (2%)
  between operations  13.7 us (2%)
    all_to_all x1, waiting for transfers between devices, local(): lax.all_to_all(built, 'tp', split_axis=0, concat_axis=0, tiled=True)  532 us
    reduce_scatter x1, waiting for transfers between devices, local(): lax.psum_scatter(jnp.dot(both_out, flat_out, preferred_element_type=jnp.f...  142 us
    all_to_all x1, starting transfers between devices, local(): lax.all_to_all(built, 'tp', split_axis=0, concat_axis=0, tiled=True)  32.7 us
  transfers between devices with their start and end apart: 4, of which 2 were waited for; matrix products, arithmetic and copies ran while one was open for 2% of the time, Pallas kernels for 0%

profile of v1, /device:TPU:38, one launch (start us, length us, event | category | flops | bytes accessed | tf_op | source)
XLA Modules:
  0.0 774.9 jit_solution(1505417734129079386)
XLA Ops:
  6.6 0.9 fusion.36
  7.4 1.1 convert_reduce_fusion
  8.5 1.2 fusion.27
  9.7 1.1 fusion.30
  10.7 3.4 tile.2
  14.2 32.7 %all-to-all-start = ((bf16[32,32,3072]{2,1,0:T(8,128)(2,1)}), bf16[32,32,3072]{2,1,0:T(8,128)(2,1)}, u32[]{:S(2)}, u32[]{:S(2)}) async-start(bf16[32,32,3072]{2,1,0:T(8,128)(2,1)} %tile.2), calls=%async_computation | async-start | bytes 12582912 | tf_op jit(solution)/shard_map/all_to_all | solution.py:87
  46.9 4.1 copy.25
  51.0 4.7 copy.11
  55.8 0.6 constant_dynamic-slice_fusion
  56.4 0.6 constant_dynamic-slice_fusion.1
  57.0 0.6 add_convert_fusion
  57.7 1.8 multiply_cosine_fusion
  59.4 532.4 %all-to-all-done = bf16[32,32,3072]{2,1,0:T(8,128)(2,1)} async-done(((bf16[32,32,3072]{2,1,0:T(8,128)(2,1)}), bf16[32,32,3072]{2,1,0:T(8,128)(2,1)}, u32[]{:S(2)}, u32[]{:S(2)}) %all-to-all-start) | async-done | bytes 6291488 | tf_op jit(solution)/shard_map/all_to_all | solution.py:87
  591.8 6.5 convolution_bitcast_fusion
  598.6 1.1 copy-done.2
  599.7 0.2 multiply_multiply_fusion
  599.9 2.1 slice.55
  602.0 2.2 slice.56
  604.2 1.7 subtract_bitcast_fusion
  605.9 0.8 copy.12
  606.8 0.3 reshape.305
  607.3 0.2 copy.19
  607.5 0.2 copy.14
  607.7 1.1 fusion.32
  608.8 0.2 copy.15
  609.0 0.2 copy.20
  609.2 5.0 while.21
  609.2 0.6 iota_compare_fusion.5
  609.8 0.5 fusion.61
  610.4 0.6 fusion.62
  610.9 0.7 fusion.63
  611.7 0.6 iota_compare_fusion.5
  612.3 0.5 fusion.61
  612.8 0.6 fusion.62
  613.4 0.7 fusion.63
  614.2 0.8 collective-permute-start.1
  615.0 5.0 while.20
  615.0 0.6 iota_compare_fusion.4
  615.6 0.5 fusion.56
  616.2 0.6 fusion.57
  616.7 0.7 fusion.58
  617.5 0.6 iota_compare_fusion.4
  618.1 0.5 fusion.56
  618.6 0.6 fusion.57
  619.2 0.7 fusion.58
  620.0 4.5 convolution_convert_fusion.2
  624.5 141.9 %reduce-scatter.2.cloned.1.call-done = bf16[32,3072]{1,0:T(8,128)(2,1)} async-done(((bf16[1024,3072]{1,0:T(8,128)(2,1)}), bf16[32,3072]{1,0:T(8,128)(2,1)}) %reduce-scatter.2.cloned.1.call-update) | async-done | bytes 196624 | tf_op jit(solution)/shard_map/reduce_scatter | solution.py:109
  766.4 1.7 fusion.33
  (30 shorter events, 0.8 us)
Async XLA Ops:
  6.5 613.4 %copy-start = (bf16[1,2,128,3072]{3,2,1,0:T(8,128)(2,1)S(1)}, bf16[1,2,128,3072]{3,2,1,0:T(8,128)(2,1)}, u32[]{:S(2)}) copy-start(bf16[1,2,128,3072]{3,2,1,0:T(8,128)(2,1)} %param.17) | copy-start | bytes 4718596
  14.2 577.6 %all-to-all-start = ((bf16[32,32,3072]{2,1,0:T(8,128)(2,1)}), bf16[32,32,3072]{2,1,0:T(8,128)(2,1)}, u32[]{:S(2)}, u32[]{:S(2)}) async-start(bf16[32,32,3072]{2,1,0:T(8,128)(2,1)} %tile.2), calls=%async_computation | async-start | bytes 12582912 | tf_op jit(solution)/shard_map/all_to_all | solution.py:87
  46.9 719.5 %reduce-scatter.2.cloned.1.call-start = ((), (), s32[]{:S(2)}) async-start(), calls=%async_computation.2 | async-start | bytes 6488064 | tf_op jit(solution)/shard_map/reduce_scatter | solution.py:109
  51.0 4.7 copy-start.3
  51.0 4.7 copy-start.4
  51.0 5.4 copy-start.5
  598.3 1.4 copy-start.2
  607.1 1.8 collective-permute-start
  614.2 5.8 collective-permute-start.1
  624.4 142.0 %copy-start.1 = (bf16[1,32,3072]{2,1,0:T(8,128)(2,1)S(1)}, bf16[1,32,3072]{2,1,0:T(8,128)(2,1)}, u32[]{:S(2)}) copy-start(bf16[1,32,3072]{2,1,0:T(8,128)(2,1)} %param.11) | copy-start | bytes 589828
Sparse Core Ops, SparseCore 0:
  624.6 141.7 reduce-scatter.1
